TPU v7x, 32 devices: a whole 2x2x4 slice. The times are simulated.
32 devices in a mesh: ep: 8 (over z, x), tp: 4 (over y, core).
Axes of the slice: x: 2, y: 2, z: 4, core: 2. Of those that a mesh axis runs over, the one named last changes fastest.
Arguments:
- tokens: bfloat16 [2048, 2880], P('ep', 'tp'), may hold values from -6 to 6
- expert_ids: int32 [2048, 4], P('ep'), may hold values from 0 to 15, all different within a row; in each aligned block of 256 rows (0 to 255, 256 to 511, ...) at most 128 rows name the same one
- combine_weights: float32 [2048, 4], P('ep'), may hold values from 0.05 to 0.6
- gate_weight: bfloat16 [16, 2880, 2880], P('ep', None, 'tp'), may hold values from -0.109375 to 0.109375
- up_weight: bfloat16 [16, 2880, 2880], P('ep', None, 'tp'), may hold values from -0.109375 to 0.109375
- down_weight: bfloat16 [16, 2880, 2880], P('ep', 'tp'), may hold values from -0.109375 to 0.109375
Outputs:
- mixed: bfloat16 [2048, 2880], P('ep', 'tp')
Inputs may be any that keep to these rules, and one draw needn't show every extreme that they name: `expert_ids`: each row names 4 different experts; within the 256 rows of one index of ep no expert is named more than 128 times, a bound that some block reaches.
All inputs are finite; a program needn't handle non-finite values.
Results may differ from a plain program's by a relative error of at most 0.014.
Values may be sent and summed in bfloat16 or wider, within the bound.
A program may use at most 128 MiB of HBM per device.

v0:
```python
import jax
import jax.numpy as jnp
from jax import lax
from jax.sharding import PartitionSpec as P


def activate(gate_acc, up_acc):
    return (up_acc + 1.0) * gate_acc * jax.nn.sigmoid(1.702 * gate_acc)


def local(tokens, expert_ids, combine_weights, gate_weight, up_weight, down_weight):
    ep_count = lax.axis_size("ep")
    exp_local = gate_weight.shape[0]
    experts = exp_local * ep_count
    tok_rows = expert_ids.shape[0]
    top_count = expert_ids.shape[1]
    capacity = 2 * tok_rows * top_count // experts
    feat_width = tokens.shape[1]
    flat_ids = expert_ids.reshape(-1)
    onehot = (flat_ids[:, None] == jnp.arange(experts, dtype=jnp.int32)[None, :]).astype(jnp.int32)
    slot_pos = jnp.sum((jnp.cumsum(onehot, axis=0) - onehot) * onehot, axis=1)
    expert_local = flat_ids % exp_local
    owner_dev = flat_ids // exp_local
    token_of = jnp.arange(tok_rows * top_count, dtype=jnp.int32) // top_count
    send_buf = jnp.zeros((exp_local, ep_count, capacity, feat_width), jnp.bfloat16)
    send_buf = send_buf.at[expert_local, owner_dev, slot_pos].set(tokens[token_of])
    arrived = lax.all_to_all(send_buf, "ep", split_axis=1, concat_axis=1, tiled=True)
    arrived = arrived.reshape(exp_local, ep_count * capacity, feat_width)
    shard_piece = lax.all_gather(arrived, "tp", axis=2, tiled=True)
    gate_new = jnp.einsum(
        "erd,edf->erf", shard_piece, gate_weight, preferred_element_type=jnp.float32
    )
    up_new = jnp.einsum("erd,edf->erf", shard_piece, up_weight, preferred_element_type=jnp.float32)
    hidden = activate(gate_new, up_new).astype(jnp.bfloat16)
    partials = jnp.einsum("erf,efd->erd", hidden, down_weight, preferred_element_type=jnp.float32)
    weights_flat = combine_weights.reshape(-1)
    summed = lax.psum_scatter(
        partials.astype(jnp.bfloat16), "tp", scatter_dimension=2, tiled=True
    ).astype(jnp.float32)
    summed = summed.reshape(exp_local, ep_count, capacity, summed.shape[2])
    returned = lax.all_to_all(
        summed.astype(jnp.bfloat16), "ep", split_axis=1, concat_axis=1, tiled=True
    ).astype(summed.dtype)
    picked = returned[expert_local, owner_dev, slot_pos]
    weighted = (picked * weights_flat[:, None]).reshape(tok_rows, top_count, picked.shape[1])
    mixed = jnp.sum(weighted, axis=1).astype(jnp.bfloat16)
    return mixed


def solution(mesh):
    in_specs = (
        P("ep", "tp"),
        P("ep", None),
        P("ep", None),
        P("ep", None, "tp"),
        P("ep", None, "tp"),
        P("ep", "tp", None),
    )
    out_specs = P("ep", "tp")
    return jax.shard_map(local, mesh=mesh, in_specs=in_specs, out_specs=out_specs, check_vma=False)
```

profile of v0, /device:TPU:0, one launch (start us, length us, event | category | flops | bytes accessed | tf_op | source)
XLA Modules:
  0.0 439.0 jit_solution(15752584724429517280)
XLA Ops:
  6.5 0.0 all-gather.2.cloned.1.call-start
  6.5 0.8 copy.44
  7.4 0.1 eq.31
  7.5 0.1 eq.27
  7.6 0.1 reshape.209
  7.8 4.5 %reduce-window.6 = s32[16,8,128]{2,1,0:T(8,128)S(1)} reduce-window(s32[16,8,128]{2,1,0:T(8,128)S(1)} %fusion.8, s32[]{:T(128)} %constant.48.clone.1), window={size=1x1x128 pad=0_0x0_0x127_0}, to_apply=%region_0.0 | reduce-window | flops 2080768 | bytes 131076 | tf_op jit(solution)/shard_map/reduce-window
  12.3 0.1 slice.13
  12.4 0.1 copy.47
  12.5 0.1 copy.48
  12.6 0.1 broadcast_add_fusion
  12.7 0.1 shift-left_or_fusion
  12.8 0.7 multiply_reduce_fusion.1
  13.5 0.7 and_reduce_fusion
  14.3 1.2 copy.49
  15.5 12.4 %scatter_custom_fusion = bf16[2048,720]{1,0:T(8,128)(2,1)S(1)} fusion(s32[1024]{0:T(1024)S(1)} %get-tuple-element.10, bf16[256,720]{1,0:T(8,128)(2,1)S(1)} %copy.49, s32[1024]{0:T(1024)S(1)} %get-tuple-element.9, bf16[]{:T(256)} %constant.47.clone.1), kind=kCustom, calls=%fused_computation.10 | custom fusion | bytes 2949122
  27.9 5.5 %copy.51 = bf16[2,8,128,720]{2,0,3,1:T(2,128)(2,1)} copy(bf16[2,8,128,720]{3,2,1,0:T(8,128)(2,1)S(1)} %bitcast.37) | data formatting | bytes 5898240 | tf_op jit(solution)/shard_map/scatter | solution.py:26
  33.5 74.4 %all_to_all.10 = bf16[2,8,128,720]{2,0,3,1:T(2,128)(2,1)S(1)} all-to-all(bf16[2,8,128,720]{2,0,3,1:T(2,128)(2,1)} %copy.51), channel_id=1, replica_groups=mesh['ep'=8,'tp'=4] {'ep'}, dimensions={1} | all-to-all | bytes 5898240 | tf_op jit(solution)/shard_map/all_to_all | solution.py:27
  107.8 1.1 copy.52
  109.0 3.3 reshape.211
  112.2 0.0 all-gather.2.cloned.1.call-update
  112.2 0.2 reduce-scatter.2.cloned.1.call-start
  112.5 76.0 %all-gather.2.cloned.1.call-done = bf16[2,1024,2880]{1,2,0:T(8,128)(2,1)} async-done(((bf16[2,1024,720]{1,2,0:T(8,128)(2,1)}), bf16[2,1024,2880]{1,2,0:T(8,128)(2,1)}) %all-gather.2.cloned.1.call-update) | async-done | bytes 11796496 | tf_op jit(solution)/shard_map/all_gather | solution.py:29
  188.5 16.2 %fusion.13 = f32[2,1024,720]{1,2,0:T(8,128)} fusion(bf16[2,2880,720]{1,2,0:T(8,128)(2,1)} %param.9, bf16[2,1024,2880]{1,2,0:T(8,128)(2,1)} %all-gather.2.cloned.1.call-done), kind=kOutput, calls=%fused_computation.43 | convolution fusion | flops 8493465600 | bytes 25989120 | tf_op jit(solution)/shard_map/erd,edf->erf/dot_general | solution.py:30
  204.6 27.0 %convolution_convert_fusion = bf16[2,1024,2880]{1,2,0:T(8,128)(2,1)} fusion(bf16[2,720,2880]{2,1,0:T(8,128)(2,1)} %param.11, f32[2,1024,720]{1,2,0:T(8,128)} %fusion.13, bf16[2,2880,720]{1,2,0:T(8,128)(2,1)} %param.10, bf16[2,1024,2880]{1,2,0:T(8,128)(2,1)} %all-gather.2.cloned.1.call-done), kind=kOutput, calls=%fused_computation.3 | convolution fusion | flops 17004625920 | bytes 46080000 | tf_op jit(solution)/shard_map/erf,efd->erd/dot_general | solution.py:35
  231.7 0.0 reduce-scatter.2.cloned.1.call-update
  231.7 0.0 copy-start
  231.7 93.6 %reduce-scatter.2.cloned.1.call-done = bf16[2,1024,720]{1,2,0:T(8,128)(2,1)} async-done(((bf16[2,1024,2880]{1,2,0:T(8,128)(2,1)}), bf16[2,1024,720]{1,2,0:T(8,128)(2,1)}) %reduce-scatter.2.cloned.1.call-update) | async-done | bytes 2949136 | tf_op jit(solution)/shard_map/reduce_scatter | solution.py:37
  325.3 4.0 copy_bitcast_fusion
  329.3 5.5 %all-to-all-start.1 = ((bf16[2,8,128,720]{2,3,0,1:T(8,128)(2,1)}), bf16[2,8,128,720]{2,3,0,1:T(8,128)(2,1)S(1)}, u32[]{:S(2)}, u32[]{:S(2)}) async-start(bf16[2,8,128,720]{2,3,0,1:T(8,128)(2,1)} %copy_bitcast_fusion), calls=%async_computation.2 | async-start | bytes 5898240 | tf_op jit(solution)/shard_map/all_to_all | solution.py:41
  334.8 0.0 copy-done
  334.8 0.1 copy.56
  335.0 66.2 %all-to-all-done.1 = bf16[2,8,128,720]{2,3,0,1:T(8,128)(2,1)S(1)} async-done(((bf16[2,8,128,720]{2,3,0,1:T(8,128)(2,1)}), bf16[2,8,128,720]{2,3,0,1:T(8,128)(2,1)S(1)}, u32[]{:S(2)}, u32[]{:S(2)}) %all-to-all-start.1) | async-done | bytes 2949152 | tf_op jit(solution)/shard_map/all_to_all | solution.py:41
  401.1 2.9 copy_convert_fusion
  404.1 6.5 %copy.55 = f32[2,8,128,720]{3,2,1,0:T(8,128)} copy(f32[2,8,128,720]{2,3,1,0:T(8,128)} %copy_convert_fusion) | data formatting | bytes 11796480 | tf_op jit(solution)/shard_map/convert_element_type | solution.py:43
  410.6 14.7 %gather_fusion = f32[1024,720]{1,0:T(8,128)S(1)} fusion(f32[2,8,128,720]{3,2,1,0:T(8,128)} %copy.55, s32[1024]{0:T(1024)S(1)} %bitcast.36), kind=kCustom, calls=%fused_computation.1 | custom fusion | bytes 5910528 | tf_op jit(solution)/shard_map/gather | solution.py:44
  425.2 2.1 gather.10
  427.4 3.9 multiply_reduce_fusion
  431.3 0.9 copy.57
  (6 shorter events, 0.1 us)
Async XLA Ops:
  6.5 181.9 %all-gather.2.cloned.1.call-start = ((), (), s32[]{:S(2)}) async-start(), calls=%async_computation.3 | async-start | bytes 14745600 | tf_op jit(solution)/shard_map/all_gather | solution.py:29
  112.2 213.1 %reduce-scatter.2.cloned.1.call-start = ((), (), s32[]{:S(2)}) async-start(), calls=%async_computation.4 | async-start | bytes 14745600 | tf_op jit(solution)/shard_map/reduce_scatter | solution.py:37
  231.7 103.1 %copy-start = (f32[256,4]{0,1:T(4,128)S(1)}, f32[256,4]{0,1:T(4,128)}, u32[]{:S(2)}) copy-start(f32[256,4]{0,1:T(4,128)} %param.8) | copy-start | bytes 12292
  329.3 71.8 %all-to-all-start.1 = ((bf16[2,8,128,720]{2,3,0,1:T(8,128)(2,1)}), bf16[2,8,128,720]{2,3,0,1:T(8,128)(2,1)S(1)}, u32[]{:S(2)}, u32[]{:S(2)}) async-start(bf16[2,8,128,720]{2,3,0,1:T(8,128)(2,1)} %copy_bitcast_fusion), calls=%async_computation.2 | async-start | bytes 5898240 | tf_op jit(solution)/shard_map/all_to_all | solution.py:41
Sparse Core Ops, SparseCore 0:
  112.4 76.0 all-gather.1
  231.8 93.4 reduce-scatter.1
where the time goes:
time: 440 us; the launch traced here: 439 us
  waiting for transfers between devices  236 us (54%)
  blocking collectives  74.4 us (17%)
  local copies, waits for them, and re-layouts  53.3 us (12%)
  matrix products  43.2 us (10%)
  between operations  13.5 us (3%)
  other arithmetic  13.1 us (3%)
  starting transfers between devices  5.73 us (1%)
    reduce_scatter x1, waiting for transfers between devices, local(): lax.psum_scatter(partials.astype(jnp.bfloat16), 'tp', scatter_dimension=2...  93.6 us
    all_gather x1, waiting for transfers between devices, local(): shard_piece = lax.all_gather(arrived, 'tp', axis=2, tiled=True)  76 us
    all_to_all x1, blocking collectives, local(): lax.all_to_all(send_buf, 'ep', split_axis=1, concat_axis=1, tiled=True)  74.4 us
    all_to_all x1, waiting for transfers between devices, local(): lax.all_to_all(summed.astype(jnp.bfloat16), 'ep', split_axis=1, concat_ax...  66.2 us
    dot_general x1, matrix products, local(): jnp.einsum('erf,efd->erd', hidden, down_weight, preferred_element_type=jn...  27 us
    gather x2, local copies, waits for them, and re-layouts, local(): picked = returned[expert_local, owner_dev, slot_pos]  16.8 us
    dot_general x1, matrix products, local(): jnp.einsum('erd,edf->erf', shard_piece, gate_weight, preferred_element_ty...  16.2 us
    unnamed x6, local copies, waits for them, and re-layouts  14.6 us
  transfers between devices with their start and end apart: 3, of which 3 were waited for; matrix products, arithmetic and copies ran while one was open for 0% of the time, Pallas kernels for 0%

commit v1 on v0

v1 whole, which is shorter than its diff:
```python
import functools

import jax
import jax.numpy as jnp
from jax import lax
from jax.experimental import pallas as pl
from jax.experimental.pallas import tpu as pltpu
from jax.sharding import PartitionSpec as P


def activate(gate_acc, up_acc):
    return (up_acc + 1.0) * gate_acc * jax.nn.sigmoid(1.702 * gate_acc)


MESH = pl.DeviceIdType.MESH


class Place:
    def __init__(self, depth):
        self.depth = depth
        e, t = lax.axis_index("ep"), lax.axis_index("tp")
        self.z, self.x, self.y, self.c = e // 2, e % 2, t // 2, t % 2

    def device(self, k=0, dx=0, dy=0, dc=0):
        ep = (self.z + k) % self.depth * 2 + (self.x + dx) % 2
        tp = (self.y + dy) % 2 * 2 + (self.c + dc) % 2
        return ep, tp

    def block(self, k=0, dx=0, dy=0, dc=0):
        ep, tp = self.device(k, dx, dy, dc)
        return ep * 4 + tp

    def greet(self):
        barrier = pltpu.get_barrier_semaphore()
        near = [self.device(k=k) for k in range(1, self.depth)]
        near += [self.device(dx=1), self.device(dy=1), self.device(dc=1)]
        for who in near:
            pl.semaphore_signal(barrier, inc=1, device_id=who, device_id_type=MESH)
        pl.semaphore_wait(barrier, len(near))


def gather_kernel(depth, own, out, lane_recv, pair_recv, lane_send, pair_send, own_sem):
    here = Place(depth)
    half = own.shape[0] // 2
    sent = []

    def piece(k, dx, dy, part):
        rows = pl.ds(part * half, half)
        if (k, dx, dy) == (0, 0, 0):
            return own.at[rows]
        return out.at[here.block(k, dx, dy), rows]

    def lane_slot(k, dx, dy):
        ep, tp = here.device(k, dx, dy)
        return ep * 2 + tp // 2

    def push(k, dx, dy, part, to):
        rows = pl.ds(part * half, half)
        copy = pltpu.make_async_remote_copy(
            src_ref=piece(k, dx, dy, part), dst_ref=out.at[here.block(k, dx, dy), rows],
            send_sem=lane_send.at[len(sent)], recv_sem=lane_recv.at[lane_slot(k, dx, dy), part],
            device_id=to, device_id_type=MESH)
        copy.start()
        sent.append(copy)

    def pair(k, dx, dy, part):
        rows = pl.ds(part * half, half)
        slot = lane_slot(k, dx, dy)
        copy = pltpu.make_async_remote_copy(
            src_ref=piece(k, dx, dy, part), dst_ref=out.at[here.block(k, dx, dy), rows],
            send_sem=pair_send.at[slot, part], recv_sem=pair_recv.at[slot, part],
            device_id=here.device(dc=1), device_id_type=MESH)
        copy.start()

    def landed(k, dx, dy, part, to):
        rows = pl.ds(part * half, half)
        ref = out.at[here.block(k, dx, dy), rows]
        pltpu.make_async_remote_copy(
            src_ref=ref, dst_ref=ref, send_sem=lane_send.at[0],
            recv_sem=lane_recv.at[lane_slot(k, dx, dy), part],
            device_id=to, device_id_type=MESH).wait_recv()

    here.greet()
    over_x, over_y = here.device(dx=1), here.device(dy=1)
    for k in range(1, depth):
        for part in (0, 1):
            push(0, 0, 0, part, here.device(k=depth - k))
    store = pltpu.make_async_copy(own, out.at[here.block()], own_sem)
    store.start()
    for k in range(depth):
        if k:
            landed(k, 0, 0, 0, here.device(k=k))
            landed(k, 0, 0, 1, here.device(k=k))
        push(k, 0, 0, 0, over_x)
        push(k, 0, 0, 1, over_y)
        push(k, 0, 0, 0, over_y)
        push(k, 0, 0, 1, over_x)
        pair(k, 0, 0, 0)
        pair(k, 0, 0, 1)
        landed(k, 1, 0, 0, over_x)
        push(k, 1, 0, 0, over_y)
        pair(k, 1, 0, 0)
        landed(k, 0, 1, 1, over_y)
        push(k, 0, 1, 1, over_x)
        pair(k, 0, 1, 1)
    for k in range(depth):
        landed(k, 0, 1, 0, over_y)
        pair(k, 0, 1, 0)
        landed(k, 1, 0, 1, over_x)
        pair(k, 1, 0, 1)
        landed(k, 1, 1, 0, over_y)
        pair(k, 1, 1, 0)
        landed(k, 1, 1, 1, over_x)
        pair(k, 1, 1, 1)
    store.wait()
    for copy in sent:
        copy.wait_send()
    for k in range(depth):
        for dx in (0, 1):
            for dy in (0, 1):
                slot = lane_slot(k, dx, dy)
                for part in (0, 1):
                    rows = pl.ds(part * half, half)
                    copy = pltpu.make_async_remote_copy(
                        src_ref=piece(k, dx, dy, part),
                        dst_ref=out.at[here.block(k, dx, dy, 1), rows],
                        send_sem=pair_send.at[slot, part], recv_sem=pair_recv.at[slot, part],
                        device_id=here.device(dc=1), device_id_type=MESH)
                    copy.wait_send()
                    copy.wait_recv()


def gather_all(tokens, ep_count, tp_count):
    rows, width = tokens.shape
    depth = ep_count // 2
    blocks = ep_count * tp_count
    sends = 2 * (depth - 1) + 6 * depth
    dma = pltpu.SemaphoreType.DMA
    return pl.pallas_call(
        functools.partial(gather_kernel, depth),
        out_shape=jax.ShapeDtypeStruct((blocks, rows, width), tokens.dtype),
        in_specs=[pl.BlockSpec(memory_space=pltpu.VMEM)],
        out_specs=pl.BlockSpec(memory_space=pl.ANY),
        scratch_shapes=[dma((blocks // 2, 2)), dma((blocks // 2, 2)), dma((sends,)),
                        dma((blocks // 2, 2)), dma(())],
        compiler_params=pltpu.CompilerParams(collective_id=0, has_side_effects=True),
    )(tokens)


def scatter_kernel(depth, part_ref, out, acc, inc, from_y, from_x, last_x, last_y, from_z,
                   load_sem, pair_send, pair_recv, send_sem, recv_sem):
    here = Place(depth)
    rows = out.shape[0]
    half = rows // 2
    low, high = pl.ds(0, half), pl.ds(half, half)
    order = list(range(1, depth)) + [0]
    spread = ((1, 1), (0, 1), (1, 0), (0, 0))
    over_x, over_y = here.device(dx=1), here.device(dy=1)
    sent = []
    loads, pairs = {}, {}
    cell = lambda k, dx, dy: (k * 2 + dx) * 2 + dy

    def add(at, part, got):
        acc[at, part] = (acc[at, part].astype(jnp.float32) + got.astype(jnp.float32)).astype(acc.dtype)

    def send(src, dst, to):
        copy = pltpu.make_async_remote_copy(
            src_ref=src, dst_ref=dst, send_sem=send_sem.at[len(sent)],
            recv_sem=recv_sem.at[len(sent)], device_id=to, device_id_type=MESH)
        copy.start()
        sent.append(copy)
        return copy

    here.greet()
    for k in order:
        for dx, dy in spread:
            i = cell(k, dx, dy)
            pairs[i] = pltpu.make_async_remote_copy(
                src_ref=part_ref.at[here.block(k, dx, dy, 1)], dst_ref=inc.at[i],
                send_sem=pair_send.at[i], recv_sem=pair_recv.at[i],
                device_id=here.device(dc=1), device_id_type=MESH)
            pairs[i].start()
            loads[i] = pltpu.make_async_copy(
                part_ref.at[here.block(k, dx, dy)], acc.at[i], load_sem.at[i])
            loads[i].start()

    wait_for = {}

    def first(k):
        for dx, dy in spread:
            i = cell(k, dx, dy)
            loads[i].wait()
            pairs[i].wait_recv()
            add(i, pl.ds(0, rows), inc[i])
            if dy:
                wait_for["y", k, dx] = send(acc.at[i, low], from_y.at[k * 2 + dx], over_y)
            if dx:
                wait_for["x", k, dy] = send(acc.at[i, high], from_x.at[k * 2 + dy], over_x)

    def second(k):
        wait_for["y", k, 1].wait_recv()
        add(cell(k, 1, 0), low, from_y[k * 2 + 1])
        wait_for["lx", k] = send(acc.at[cell(k, 1, 0), low], last_x.at[k], over_x)
        wait_for["x", k, 1].wait_recv()
        add(cell(k, 0, 1), high, from_x[k * 2 + 1])
        wait_for["ly", k] = send(acc.at[cell(k, 0, 1), high], last_y.at[k], over_y)
        wait_for["y", k, 0].wait_recv()
        add(cell(k, 0, 0), low, from_y[k * 2])
        wait_for["x", k, 0].wait_recv()
        add(cell(k, 0, 0), high, from_x[k * 2])

    def third(k):
        wait_for["lx", k].wait_recv()
        add(cell(k, 0, 0), low, last_x[k])
        wait_for["ly", k].wait_recv()
        add(cell(k, 0, 0), high, last_y[k])
        if k:
            wait_for["z", k] = send(acc.at[cell(k, 0, 0)], from_z.at[k - 1], here.device(k=k))

    for i in range(depth + 2):
        if i < depth:
            first(order[i])
        if 0 <= i - 1 < depth:
            second(order[i - 1])
        if 0 <= i - 2:
            third(order[i - 2])
    total = acc[0].astype(jnp.float32)
    for k in range(1, depth):
        wait_for["z", k].wait_recv()
        total = total + from_z[k - 1].astype(jnp.float32)
    out[...] = total.astype(out.dtype)
    for copy in sent:
        copy.wait_send()
    for copy in pairs.values():
        copy.wait_send()


def scatter_sum(partial, ep_count):
    blocks, rows, width = partial.shape
    depth = ep_count // 2
    lane, half = blocks // 2, rows // 2
    sends = 6 * depth + depth - 1
    dma, kind = pltpu.SemaphoreType.DMA, partial.dtype
    return pl.pallas_call(
        functools.partial(scatter_kernel, depth),
        out_shape=jax.ShapeDtypeStruct((rows, width), kind),
        in_specs=[pl.BlockSpec(memory_space=pl.ANY)],
        out_specs=pl.BlockSpec(memory_space=pltpu.VMEM),
        scratch_shapes=[
            pltpu.VMEM((lane, rows, width), kind), pltpu.VMEM((lane, rows, width), kind),
            pltpu.VMEM((2 * depth, half, width), kind), pltpu.VMEM((2 * depth, half, width), kind),
            pltpu.VMEM((depth, half, width), kind), pltpu.VMEM((depth, half, width), kind),
            pltpu.VMEM((depth - 1, rows, width), kind),
            dma((lane,)), dma((lane,)), dma((lane,)), dma((sends,)), dma((sends,)),
        ],
        compiler_params=pltpu.CompilerParams(
            collective_id=1, has_side_effects=True, vmem_limit_bytes=48 * 1024 * 1024),
    )(partial)


def local(tokens, expert_ids, combine_weights, gate_weight, up_weight, down_weight):
    ep_count = lax.axis_size("ep")
    tp_count = lax.axis_size("tp")
    exp_local = gate_weight.shape[0]
    experts = exp_local * ep_count
    tok_rows = expert_ids.shape[0]
    top_count = expert_ids.shape[1]
    capacity = 2 * tok_rows * top_count // experts
    feat_width = tokens.shape[1]
    ff_width = gate_weight.shape[2]
    width = feat_width * tp_count
    f32, bf16 = jnp.float32, jnp.bfloat16

    ids_all = lax.all_gather(expert_ids.T, "ep")
    weights_all = lax.all_gather(combine_weights.T, "ep")
    first = lax.axis_index("ep") * exp_local
    mine = first + jnp.arange(exp_local, dtype=jnp.int32)
    hit = ids_all[:, None, :, :] == mine[None, :, None, None]
    chosen = jnp.any(hit, axis=2)
    weight = jnp.sum(jnp.where(hit, weights_all[:, None, :, :], 0.0), axis=2)

    ahead = jnp.triu(jnp.ones((tok_rows, tok_rows), bf16), 1)
    slot = lax.dot_general(
        chosen.reshape(-1, tok_rows).astype(bf16), ahead, (((1,), (0,)), ((), ())),
        preferred_element_type=f32,
    ).astype(jnp.int32).reshape(chosen.shape)
    place = jnp.where(chosen, slot, -1)
    take = place[:, :, None, :] == jnp.arange(capacity, dtype=jnp.int32)[None, None, :, None]
    slot_weight = jnp.sum(jnp.where(take, weight[:, :, None, :], 0.0), axis=3)
    take = take.astype(bf16)

    paired = tp_count == 2 * 2 and ep_count % 2 == 0
    spread = gather_all(tokens, ep_count, tp_count) if paired else lax.all_gather(
        tokens, ("ep", "tp")
    )
    gathered = spread.reshape(
        ep_count, tp_count, tok_rows, feat_width
    )
    routed = jnp.einsum(
        "sect,sjtf->escjf", take, gathered, preferred_element_type=f32
    ).astype(bf16)
    rows = routed.reshape(exp_local, ep_count * capacity, width)
    gate_new = jnp.einsum("erd,edf->erf", rows, gate_weight, preferred_element_type=f32)
    up_new = jnp.einsum("erd,edf->erf", rows, up_weight, preferred_element_type=f32)
    row_weight = slot_weight.transpose(1, 0, 2).reshape(exp_local, ep_count * capacity, 1)
    hidden = (activate(gate_new, up_new) * row_weight).astype(bf16)
    expert_out = jnp.einsum(
        "erf,efd->erd", hidden, down_weight, preferred_element_type=f32
    ).astype(bf16)
    expert_out = expert_out.reshape(exp_local, ep_count, capacity, tp_count, feat_width)
    partial = jnp.einsum(
        "sect,escjf->sjtf", take, expert_out, preferred_element_type=f32
    ).astype(bf16)
    partial = partial.reshape(ep_count * tp_count, tok_rows, feat_width)
    if paired:
        return scatter_sum(partial, ep_count)
    mixed = lax.psum_scatter(partial, ("ep", "tp"), scatter_dimension=0, tiled=True)
    return mixed.reshape(tok_rows, feat_width)


def solution(mesh):
    in_specs = (
        P("ep", "tp"),
        P("ep", None),
        P("ep", None),
        P("ep", None, "tp"),
        P("ep", None, "tp"),
        P("ep", "tp", None),
    )
    out_specs = P("ep", "tp")
    return jax.shard_map(local, mesh=mesh, in_specs=in_specs, out_specs=out_specs, check_vma=False)
```

time: 440 us -> 344 us (0.78)
  waiting for transfers between devices: 236 us -> 0 us
  Pallas kernels: 0 us -> 132 us
  matrix products: 43.2 us -> 72.7 us
  local copies, waits for them, and re-layouts: 53.3 us -> 73.3 us
  between operations: 13.5 us -> 0.08 us
  other arithmetic: 13.1 us -> 0.59 us
  blocking collectives: 74.4 us -> 63.3 us
  starting transfers between devices: 5.73 us -> 0 us
    pallas_call x0 -> x2, Pallas kernels: none -> 132 us  [the longest x1 67.1 us: scatter_sum(): pl.pallas_call(functools.partial(scatter_kernel, depth), out_shape=jax.Sh...]
    reduce_scatter x1 -> x0, waiting for transfers between devices: 93.6 us -> none  [local(): lax.psum_scatter(partials.astype(jnp.bfloat16), 'tp', scatter_dimension=2...]
    all_gather x1 -> x0, waiting for transfers between devices: 76 us -> none  [local(): shard_piece = lax.all_gather(arrived, 'tp', axis=2, tiled=True)]
    all_to_all x1 -> x0, blocking collectives: 74.4 us -> none  [local(): lax.all_to_all(send_buf, 'ep', split_axis=1, concat_axis=1, tiled=True)]
    all_to_all x1 -> x0, waiting for transfers between devices: 66.2 us -> none  [local(): lax.all_to_all(summed.astype(jnp.bfloat16), 'ep', split_axis=1, concat_ax...]
    all_gather x0 -> x2, blocking collectives: none -> 63.3 us  [the longest x1 32.5 us: local(): ids_all = lax.all_gather(expert_ids.T, 'ep')]
    convert_element_type x2, local copies, waits for them, and re-layouts: 10.5 us -> 40.6 us  [the longest x1 24.3 us: local(): routed = jnp.einsum('sect,sjtf->escjf', take, gathered, preferred_element...]
    dot_general x2 -> x5, matrix products: 43.2 us -> 72.7 us  [the longest x1 27.2 us: local(): jnp.einsum('erf,efd->erd', hidden, down_weight, preferred_element_type=f32)]
  transfers between devices with their start and end apart: 3 -> 0, of which waited for: 3 -> 0; matrix products, arithmetic and copies ran while one was open for 0% -> 0% of each run, Pallas kernels for 0% -> 0%
where the time goes in v1:
time: 344 us; the launch traced here: 342 us
  Pallas kernels  132 us (38%)
  local copies, waits for them, and re-layouts  73.3 us (21%)
  matrix products  72.7 us (21%)
  blocking collectives  63.3 us (18%)
    pallas_call x1, Pallas kernels, scatter_sum(): pl.pallas_call(functools.partial(scatter_kernel, depth), out_shape=jax.Sh...  67.1 us
    pallas_call x1, Pallas kernels, gather_all(): pl.pallas_call(functools.partial(gather_kernel, depth), out_shape=jax.Sha...  65.2 us
    all_gather x1, blocking collectives, local(): ids_all = lax.all_gather(expert_ids.T, 'ep')  32.5 us
    all_gather x1, blocking collectives, local(): weights_all = lax.all_gather(combine_weights.T, 'ep')  30.7 us
    dot_general x1, matrix products, local(): jnp.einsum('erf,efd->erd', hidden, down_weight, preferred_element_type=f32)  27.2 us
    convert_element_type x1, local copies, waits for them, and re-layouts, local(): routed = jnp.einsum('sect,sjtf->escjf', take, gathered, preferred_element...  24.3 us
    reshape x1, local copies, waits for them, and re-layouts, local(): rows = routed.reshape(exp_local, ep_count * capacity, width)  18.5 us
    convert_element_type x1, local copies, waits for them, and re-layouts, local(): partial = jnp.einsum('sect,escjf->sjtf', take, expert_out, preferred_elem...  16.3 us

profile of v1, /device:TPU:0, one launch (start us, length us, event | category | flops | bytes accessed | tf_op | source)
XLA Modules:
  0.0 342.3 jit_solution(12794418423876645274)
XLA Ops:
  0.0 32.5 %all-gather.2 = s32[8,4,256]{2,1,0:T(4,128)S(1)} all-gather(s32[1,4,256]{2,1,0:T(4,128)} %bitcast.55), channel_id=2, replica_groups=mesh['ep'=8,'tp'=4] {'ep'}, dimensions={0}, use_global_device_ids=true | all-gather | bytes 36864 | tf_op jit(solution)/shard_map/all_gather | solution.py:274
  32.6 0.1 compare_reduce_fusion
  32.7 0.1 convolution_convert_fusion.1
  32.9 30.7 %all-gather.3 = f32[8,4,256]{2,1,0:T(4,128)S(1)} all-gather(f32[1,4,256]{2,1,0:T(4,128)} %bitcast.56), channel_id=3, replica_groups=mesh['ep'=8,'tp'=4] {'ep'}, dimensions={0}, use_global_device_ids=true | all-gather | bytes 36864 | tf_op jit(solution)/shard_map/all_gather | solution.py:275
  63.7 0.1 fusion.16
  63.7 0.4 select_reduce_fusion
  64.2 1.9 copy.28.own
  66.1 65.2 %shard_map.64 = bf16[32,256,720]{2,1,0:T(8,128)(2,1)} custom-call(bf16[256,720]{1,0:T(8,128)(2,1)} %copy.28.own), custom_call_target="tpu_custom_call" | custom-call | tf_op jit(solution)/shard_map/pallas_call | solution.py:139
  131.3 15.0 %convert_bitcast_fusion = bf16[2,8,128,4,720]{2,4,3,0,1:T(8,128)(2,1)} fusion(bf16[8,4,256,720,1]{3,2,1,4,0:T(8,128)(2,1)} %bitcast.50, s32[8,2,256]{2,1,0:T(2,128)S(1)} %copy.27), kind=kOutput, calls=%fused_computation.4 | convolution fusion | flops 3026321408 | bytes 23609344 | tf_op jit(solution)/shard_map/sect,sjtf->escjf/dot_general | solution.py:299
  146.4 24.3 %copy.30 = bf16[2,8,128,4,720]{2,1,4,3,0:T(8,128)(2,1)} copy(bf16[2,8,128,4,720]{2,4,3,0,1:T(8,128)(2,1)} %convert_bitcast_fusion) | data formatting | bytes 23592960 | tf_op jit(solution)/shard_map/convert_element_type | solution.py:301
  170.7 18.5 %reshape.37 = bf16[2,1024,2880]{1,2,0:T(8,128)(2,1)} reshape(bf16[2,8,128,4,720]{2,1,4,3,0:T(8,128)(2,1)} %copy.30) | data formatting | bytes 23592960 | tf_op jit(solution)/shard_map/reshape | solution.py:302
  189.2 16.2 %fusion.25 = f32[2,1024,720]{1,2,0:T(8,128)} fusion(bf16[2,2880,720]{1,2,0:T(8,128)(2,1)} %param.9, bf16[2,1024,2880]{1,2,0:T(8,128)(2,1)} %reshape.37), kind=kOutput, calls=%fused_computation.31 | convolution fusion | flops 8493465600 | bytes 25989120 | tf_op jit(solution)/shard_map/erd,edf->erf/dot_general | solution.py:303
  205.3 27.2 %convolution_convert_fusion = bf16[2,1024,2880]{1,2,0:T(8,128)(2,1)} fusion(bf16[2,720,2880]{2,1,0:T(8,128)(2,1)} %param.11, f32[2,1024,720]{1,2,0:T(8,128)} %fusion.25, f32[2,1024]{1,0:T(2,128)S(1)} %bitcast.54, bf16[2,2880,720]{1,2,0:T(8,128)(2,1)} %param.10, bf16[2,1024,2880]{1,2,0:T(8,128)(2,1)} %reshape.37), kind=kOutput, calls=%fused_computation.5 | convolution fusion | flops 17006100480 | bytes 46088192 | tf_op jit(solution)/shard_map/erf,efd->erd/dot_general | solution.py:307
  232.5 11.3 %copy.42 = bf16[720,8,8,128]{3,2,1,0:T(8,128)(2,1)} copy(bf16[720,8,8,128]{3,1,2,0:T(8,128)(2,1)} %bitcast.53) | data formatting | bytes 23592960
  243.8 14.2 %fusion = bf16[8,4,256,720]{2,3,1,0:T(8,128)(2,1)} fusion(bf16[2,8,128,4,720]{2,1,4,3,0:T(8,128)(2,1)} %bitcast.52, s32[8,2,256]{2,1,0:T(2,128)S(1)} %copy.27), kind=kOutput, calls=%fused_computation.1 | convolution fusion | flops 3026321408 | bytes 23609344 | tf_op jit(solution)/shard_map/sect,escjf->sjtf/dot_general | solution.py:311
  258.0 16.3 %copy.34 = bf16[8,4,256,720]{3,2,1,0:T(8,128)(2,1)} copy(bf16[8,4,256,720]{2,3,1,0:T(8,128)(2,1)} %fusion) | data formatting | bytes 23592960 | tf_op jit(solution)/shard_map/convert_element_type | solution.py:313
  274.3 67.1 %shard_map.65 = bf16[256,720]{1,0:T(8,128)(2,1)S(1)} custom-call(bf16[32,256,720]{2,1,0:T(8,128)(2,1)} %bitcast.51), custom_call_target="tpu_custom_call" | custom-call | tf_op jit(solution)/shard_map/pallas_call | solution.py:244
  341.4 0.9 copy.35
  (9 shorter events, 0.1 us)
